TPU v7x, 32 devices: a whole 2x2x4 slice. The times are simulated.
32 devices in a mesh: sector: 4 (over y, x), obl: 8 (over z, core).
Axes of the slice: x: 2, y: 2, z: 4, core: 2. Of those that a mesh axis runs over, the one named last changes fastest.
Arguments:
- spectrum: float32 [2, 8, 8, 65536], P(None, None, 'sector', 'obl'), may hold values from -6 to 6
- quantile_index: int32 [8], replicated, may hold values from 32768 to 64512
- bands: int32 [131072], P(('sector', 'obl')), may hold values from 1 to 1024
- default_prob: float32 [131072], P(('sector', 'obl')), may hold values from 0.002 to 0.1
- weights: int32 [8, 131072], P(None, ('sector', 'obl')), may hold values from 0 to 8
- live_rows: int32 [4, 8], P('sector', 'obl'), may hold values from 1 to 4096, as said below
Outputs:
- obligor_contrib: float32 [8, 131072], P(None, ('sector', 'obl'))
- sector_share: float32 [8, 8], P(None, 'sector')
Inputs may be any that keep to these rules, and one draw needn't show every extreme that they name: `live_rows`: in each row (the devices of one sector index), the entries sum to 8192; exactly one of them equals 4096.
All inputs are finite; a program needn't handle non-finite values.
Results may differ from a plain program's by a relative error of at most 0.00011.
Values sent between devices are 32-bit elements; how exact they have to be, the bound alone decides.
A program may use at most 64 MiB of HBM per device.

v0:
```python
import math

import jax
import jax.numpy as jnp
from jax import lax
from jax.sharding import PartitionSpec as P

RAD = 256
BANDS = 1024
OBL_DEV = 1024


def phase_tables(rows_index, cols_index, radix):
    angle = (rows_index[:, None] * cols_index[None, :] % radix).astype(jnp.float32) * (
        2.0 * math.pi / radix
    )
    return (jnp.cos(angle), jnp.sin(angle))


def first_section(real_part, imag_part, rows_index, cols_index, radix):
    cosine, sine_table = phase_tables(rows_index, cols_index, radix)
    highest = lax.Precision.HIGHEST
    out_real = jnp.einsum("kab,ac->ckb", real_part, cosine, precision=highest) - jnp.einsum(
        "kab,ac->ckb", imag_part, sine_table, precision=highest
    )
    out_imag = jnp.einsum("kab,ac->ckb", real_part, sine_table, precision=highest) + jnp.einsum(
        "kab,ac->ckb", imag_part, cosine, precision=highest
    )
    return (out_real, out_imag)


def second_section(first_real, first_imag, cols_index, radix):
    grid_size = radix * radix
    b_index = jnp.arange(radix, dtype=jnp.int32)
    twist = (cols_index[:, None] * b_index[None, :]).astype(jnp.float32) * (
        2.0 * math.pi / grid_size
    )
    twist_cos = jnp.cos(twist)[:, None, :]
    twist_sin = jnp.sin(twist)[:, None, :]
    turned_real = first_real * twist_cos - first_imag * twist_sin
    turned_imag = first_real * twist_sin + first_imag * twist_cos
    cosine, sine_table = phase_tables(b_index, b_index, radix)
    highest = lax.Precision.HIGHEST
    loss_field = jnp.einsum("ckb,bd->kdc", turned_real, cosine, precision=highest) - jnp.einsum(
        "ckb,bd->kdc", turned_imag, sine_table, precision=highest
    )
    return loss_field / grid_size


def whole_rows(loss_field, quantiles, band_count):
    grid_size = loss_field.shape[1]
    positions = jnp.arange(grid_size, dtype=jnp.int32)
    upper_tail = jnp.sum(
        jnp.where(positions[None, :] >= quantiles[:, None], loss_field, 0.0), axis=1
    )
    index_table = (quantiles - band_count)[:, None] + jnp.arange(band_count, dtype=jnp.int32)[
        None, :
    ]
    window = jnp.take_along_axis(loss_field, index_table, axis=1)
    return (upper_tail, window)


def tail_lookup(all_tables, scaled, band_rows):
    scen_count, sectors_all, band_count = all_tables.shape
    row_total = band_rows.shape[0]
    block_size = math.gcd(row_total, 512)
    flat_tables = all_tables.reshape(scen_count * sectors_all, band_count)
    band_offsets = jnp.arange(band_count, dtype=jnp.int32)
    highest = lax.Precision.HIGHEST

    def block_step(block_turn, running):
        contrib, partial_value = running
        block_start = block_turn * block_size
        band_block = lax.dynamic_slice_in_dim(band_rows, block_start, block_size, 0)
        scaled_block = lax.dynamic_slice_in_dim(scaled, block_start, block_size, 1)
        one_hot = (band_offsets[:, None] == band_block[None, :]).astype(jnp.float32)
        looked = jnp.dot(flat_tables, one_hot, precision=highest).reshape(
            scen_count, sectors_all, block_size
        )
        product = scaled_block[None, :, :] * looked
        contrib = lax.dynamic_update_slice_in_dim(contrib, jnp.sum(product, axis=1), block_start, 1)
        return (contrib, partial_value + jnp.sum(product, axis=2))

    initial = (
        jnp.zeros((scen_count, row_total), jnp.float32),
        jnp.zeros((scen_count, sectors_all), jnp.float32),
    )
    return lax.fori_loop(0, row_total // block_size, block_step, initial)


def on_device(spectrum, quantile_index, bands, default_prob, weights, live_rows):
    scen_count = spectrum.shape[1]
    sec_local = spectrum.shape[2]
    batch_rows = scen_count * sec_local
    radix = RAD
    grid_size = radix * radix
    obl_count = lax.axis_size("obl")
    quantiles = jnp.repeat(quantile_index, sec_local)
    band_offsets = jnp.arange(BANDS, dtype=jnp.int32)
    highest = lax.Precision.HIGHEST
    upper_tri = (band_offsets[:, None] + band_offsets[None, :] >= BANDS - 1).astype(jnp.float32)
    full_index = jnp.arange(radix, dtype=jnp.int32)
    flat_spectra = spectrum.reshape(2, batch_rows, grid_size // obl_count)
    mine = lax.all_to_all(flat_spectra, "obl", split_axis=1, concat_axis=2, tiled=True)
    my_rows = batch_rows // obl_count
    mine = mine.reshape(2, my_rows, radix, radix)
    first_real, first_imag = first_section(mine[0], mine[1], full_index, full_index, radix)
    loss_field = second_section(first_real, first_imag, full_index, radix).reshape(
        my_rows, grid_size
    )
    my_quantiles = lax.dynamic_slice_in_dim(quantiles, lax.axis_index("obl") * my_rows, my_rows, 0)
    upper_tail, window = whole_rows(loss_field, my_quantiles, BANDS)
    my_tables = upper_tail[:, None] + jnp.dot(window, upper_tri, precision=highest)
    tables = lax.all_gather(my_tables, "obl", axis=0, tiled=True).reshape(
        scen_count, sec_local, BANDS
    )
    all_tables = lax.all_gather(tables, "sector", axis=1, tiled=True)
    live_count = live_rows[0, 0]
    cap_rows = bands.shape[0]
    live_mask = jnp.arange(cap_rows, dtype=jnp.int32) < live_count
    exposure = bands.astype(jnp.float32)
    scaled = jnp.where(
        live_mask[None, :],
        weights.astype(jnp.float32) * (default_prob * exposure / 256.0)[None, :],
        0.0,
    )
    obligor_contrib, partial_value = tail_lookup(
        all_tables, scaled, jnp.where(live_mask, bands - 1, 0)
    )
    sector_part = lax.psum_scatter(partial_value, "sector", scatter_dimension=1, tiled=True)
    sector_total = lax.psum(sector_part, "obl")
    obligors = OBL_DEV * lax.axis_size("sector") * obl_count
    sector_share = sector_total * (all_tables.shape[1] / obligors)
    return (obligor_contrib, sector_share)


def solution(mesh):
    in_specs = (
        P(None, None, "sector", "obl"),
        P(),
        P(("sector", "obl")),
        P(("sector", "obl")),
        P(None, ("sector", "obl")),
        P("sector", "obl"),
    )
    out_specs = (P(None, ("sector", "obl")), P(None, "sector"))
    return jax.shard_map(
        on_device, mesh=mesh, in_specs=in_specs, out_specs=out_specs, check_vma=False
    )
```

profile of v0, /device:TPU:0, one launch (start us, length us, event | category | flops | bytes accessed | tf_op | source)
XLA Modules:
  0.0 129.3 jit_solution(12231108060849886183)
XLA Ops:
  0.6 3.2 %copy.36 = f32[2,8,2,8192]{3,0,2,1:T(2,128)} copy(f32[2,8,2,8192]{3,2,1,0:T(2,128)} %param.8) | data formatting | bytes 2097152 | tf_op jit(solution)/shard_map/reshape | solution.py:103
  3.8 6.4 %all-to-all-start = ((f32[2,16,8192]{2,0,1:T(2,128)}), f32[2,16,8192]{2,0,1:T(2,128)S(1)}, u32[]{:S(2)}, u32[]{:S(2)}) async-start(f32[2,16,8192]{2,0,1:T(2,128)} %bitcast.2), calls=%async_computation | async-start | bytes 2097152 | tf_op jit(solution)/shard_map/all_to_all | solution.py:104
  15.9 20.8 %all-to-all-done = f32[2,16,8192]{2,0,1:T(2,128)S(1)} async-done(((f32[2,16,8192]{2,0,1:T(2,128)}), f32[2,16,8192]{2,0,1:T(2,128)S(1)}, u32[]{:S(2)}, u32[]{:S(2)}) %all-to-all-start) | async-done | bytes 1048608 | tf_op jit(solution)/shard_map/all_to_all | solution.py:104
  36.7 1.1 fusion.87
  38.2 1.6 %fusion.28 = f32[256,2,256]{2,0,1:T(8,128)S(1)} fusion(f32[2,256,256]{2,1,0:T(8,128)S(1)} %squeeze.10), kind=kOutput, calls=%fused_computation.42 | convolution fusion | flops 403570688 | bytes 1048576 | tf_op jit(solution)/shard_map/kab,ac->ckb/dot_general | solution.py:23
  39.9 1.6 %fusion.23 = f32[256,2,256]{2,0,1:T(8,128)S(1)} fusion(f32[2,256,256]{2,1,0:T(8,128)S(1)} %squeeze.10), kind=kOutput, calls=%fused_computation.37 | convolution fusion | flops 403570688 | bytes 1048576 | tf_op jit(solution)/shard_map/kab,ac->ckb/dot_general | solution.py:26
  41.9 1.6 %convolution_subtract_fusion.1 = f32[256,2,256]{2,0,1:T(8,128)S(1)} fusion(f32[256,2,256]{2,0,1:T(8,128)S(1)} %fusion.28, f32[2,256,256]{2,1,0:T(8,128)S(1)} %squeeze.11), kind=kOutput, calls=%fused_computation.18 | convolution fusion | flops 403701760 | bytes 1572864 | tf_op jit(solution)/shard_map/kab,ac->ckb/dot_general | solution.py:23
  43.5 1.6 %convolution_add_fusion = f32[256,2,256]{2,0,1:T(8,128)S(1)} fusion(f32[256,2,256]{2,0,1:T(8,128)S(1)} %fusion.23, f32[2,256,256]{2,1,0:T(8,128)S(1)} %squeeze.11), kind=kOutput, calls=%fused_computation.17 | convolution fusion | flops 403701760 | bytes 1572864 | tf_op jit(solution)/shard_map/kab,ac->ckb/dot_general | solution.py:26
  45.2 1.7 %fusion.15 = f32[256,256,2]{1,0,2:T(8,128)S(1)} fusion(f32[256,2,256]{2,0,1:T(8,128)S(1)} %convolution_add_fusion, f32[256,2,256]{2,0,1:T(8,128)S(1)} %convolution_subtract_fusion.1, f32[256,256]{1,0:T(8,128)S(1)} %copy.32, f32[256,256]{1,0:T(8,128)S(1)} %copy.31), kind=kOutput, calls=%fused_computation.26 | convolution fusion | flops 403963904 | bytes 2097152 | tf_op jit(solution)/shard_map/ckb,bd->kdc/dot_general | solution.py:44
  46.9 2.0 %fusion.11 = (f32[2]{0:T(128)S(1)}, f32[256,256,2]{1,0,2:T(8,128)S(1)}) fusion(s32[256,256]{1,0:T(8,128)S(1)} %copy.27, s32[2]{0:T(128)S(1)} %copy-done.4, f32[256,256,2]{1,0,2:T(8,128)S(1)} %fusion.15, f32[256,2,256]{2,0,1:T(8,128)S(1)} %convolution_add_fusion, f32[256,2,256]{2,0,1:T(8,128)S(1)} %convolution_subtract_fusion.1, f32[256,256]{1,0:T(8,128)S(1)} %copy.32, ...), kind=kOutput, calls=%fused_computation.22 | convolution fusion | flops 404619264 | bytes 2883600 | tf_op jit(solution)/shard_map/ckb,bd->kdc/dot_general | solution.py:44
  49.4 17.7 %gather_fusion = f32[2048]{0:T(1024)S(1)} fusion(f32[2,65536]{1,0:T(2,128)S(1)} %bitcast.69, s32[2048]{0:T(1024)S(1)} %bitcast.70), kind=kCustom, calls=%fused_computation | custom fusion | bytes 32768 | tf_op jit(solution)/shard_map/jit(take_along_axis)/gather | solution.py:59
  67.8 14.0 %all-gather = f32[8,2,1024]{2,1,0:T(2,128)S(1)} all-gather(f32[1,2,1024]{2,1,0:T(2,128)S(1)} %fusion.10), channel_id=1, replica_groups=mesh['sector'=4,'obl'=8] {'obl'}, dimensions={0}, use_global_device_ids=true | all-gather | bytes 73728 | tf_op jit(solution)/shard_map/all_gather | solution.py:114
  81.8 9.0 %all_gather.7 = f32[8,8,1024]{2,0,1:T(8,128)S(1)} all-gather(f32[8,2,1024]{2,0,1:T(8,128)S(1)} %copy.33), channel_id=1, replica_groups=mesh['sector'=4,'obl'=8] {'sector'}, dimensions={1}, use_global_device_ids=true | all-gather | bytes 327680 | tf_op jit(solution)/shard_map/all_gather | solution.py:117
  91.0 15.1 %while.16 = (s32[]{:T(128)}, f32[8,4096]{1,0:T(8,128)S(1)}, f32[8,8]{1,0:T(8,128)S(1)}, f32[8,4096]{1,0:T(8,128)S(1)}, s32[4096]{0:T(1024)}, /*index=5*/f32[64,1...) while((s32[]{:T(128)}, f32[8,4096]{1,0:T(8,128)S(1)}, f32[8,8]{1,0:T(8,128)S(1)}, ...), condition=%wide.region_4.5_spmd.clone, body=%wide.region_1.4_spmd.clone.sunk | while | flops 403304512 | bytes 646825 | solution.py:88
  91.8 0.9 fusion.97
  93.7 0.9 fusion.97
  95.6 0.9 fusion.97
  97.5 0.9 fusion.97
  99.4 0.9 fusion.97
  101.3 0.9 fusion.97
  103.1 0.9 fusion.97
  105.0 0.9 fusion.97
  106.2 8.9 %all-reduce = f32[8,8]{0,1:T(8,128)S(1)} all-reduce(f32[8,8]{0,1:T(8,128)S(1)} %copy.35), channel_id=2, replica_groups=mesh['sector'=4,'obl'=8] {'sector'}, use_global_device_ids=true, to_apply=%region_5.6.clone | all-reduce | flops 64 | bytes 512
  115.1 13.6 %psum.7 = f32[8,2]{0,1:T(2,128)S(1)} all-reduce(f32[8,2]{0,1:T(2,128)S(1)} %constant_dynamic-slice_fusion.1), channel_id=1, replica_groups=mesh['sector'=4,'obl'=8] {'obl'}, use_global_device_ids=true, to_apply=%region_6.7 | all-reduce | flops 16 | bytes 128 | tf_op jit(solution)/shard_map/psum | solution.py:131
  (92 shorter events, 15.0 us)
Async XLA Ops:
  3.8 32.9 %all-to-all-start = ((f32[2,16,8192]{2,0,1:T(2,128)}), f32[2,16,8192]{2,0,1:T(2,128)S(1)}, u32[]{:S(2)}, u32[]{:S(2)}) async-start(f32[2,16,8192]{2,0,1:T(2,128)} %bitcast.2), calls=%async_computation | async-start | bytes 2097152 | tf_op jit(solution)/shard_map/all_to_all | solution.py:104
  10.1 2.1 %copy-start.5 = (s32[8]{0:T(128)S(1)}, s32[8]{0:T(128)}, u32[]{:S(2)}) copy-start(s32[8]{0:T(128)} %param.9) | copy-start | bytes 100
  11.0 3.0 %copy-start.6 = (u32[32]{0:T(128)S(1)}, u32[32]{0:T(128)}, u32[]{:S(2)}) copy-start(u32[32]{0:T(128)} %constant.118) | copy-start | bytes 388
  11.0 4.2 %copy-start.2 = (s32[4096]{0:T(1024)S(1)}, s32[4096]{0:T(1024)}, u32[]{:S(2)}) copy-start(s32[4096]{0:T(1024)} %param.10) | copy-start | bytes 49156
  11.0 4.8 %copy-start.3 = (f32[4096]{0:T(1024)S(1)}, f32[4096]{0:T(1024)}, u32[]{:S(2)}) copy-start(f32[4096]{0:T(1024)} %param.11) | copy-start | bytes 49156
  11.9 4.0 %copy-start = (s32[8,4096]{1,0:T(8,128)S(1)}, s32[8,4096]{1,0:T(8,128)}, u32[]{:S(2)}) copy-start(s32[8,4096]{1,0:T(8,128)} %param.12) | copy-start | bytes 393220
  45.2 1.7 %copy-start.4 = (s32[2]{0:T(128)S(1)}, s32[2]{0:T(128)}, u32[]{:S(2)}) copy-start(s32[2]{0:T(128)} %get-tuple-element.165) | copy-start | bytes 28
  106.1 23.2 %copy-start.1 = (f32[8,4096]{1,0:T(8,128)}, f32[8,4096]{1,0:T(8,128)S(1)}, u32[]{:S(2)}) copy-start(f32[8,4096]{1,0:T(8,128)S(1)} %get-tuple-element.125) | copy-start | bytes 393220
where the time goes:
time: 130 us; the launch traced here: 129 us
  blocking collectives  45.5 us (35%)
  local copies, waits for them, and re-layouts  31.5 us (24%)
  waiting for transfers between devices  20.8 us (16%)
  matrix products  18.1 us (14%)
  starting transfers between devices  6.35 us (5%)
  other arithmetic  4.68 us (4%)
  between operations  2.22 us (2%)
    all_to_all x1, waiting for transfers between devices, on_device(): lax.all_to_all(flat_spectra, 'obl', split_axis=1, concat_axis=2, tiled=True)  20.8 us
    gather x2, local copies, waits for them, and re-layouts, whole_rows(): window = jnp.take_along_axis(loss_field, index_table, axis=1)  17.7 us
    all_gather x1, blocking collectives, on_device(): lax.all_gather(my_tables, 'obl', axis=0, tiled=True)  14 us
    psum x1, blocking collectives, on_device(): sector_total = lax.psum(sector_part, 'obl')  13.6 us
    all_gather x1, blocking collectives, on_device(): all_tables = lax.all_gather(tables, 'sector', axis=1, tiled=True)  8.99 us
    unnamed x1, blocking collectives  8.9 us
    dot_general x8, matrix products, block_step(): jnp.dot(flat_tables, one_hot, precision=highest)  7.05 us
    all_to_all x1, starting transfers between devices, on_device(): lax.all_to_all(flat_spectra, 'obl', split_axis=1, concat_axis=2, tiled=True)  6.35 us
  transfers between devices with their start and end apart: 1, of which 1 were waited for; matrix products, arithmetic and copies ran while one was open for 3% of the time, Pallas kernels for 0%

commit v1 on v0

v1 whole, which is shorter than its diff:
```python
import functools
import math

import jax
import jax.numpy as jnp
import numpy as np
from jax import lax
from jax.experimental import pallas as pl
from jax.experimental.pallas import tpu as pltpu
from jax.sharding import PartitionSpec as P

BANDS = 1024
OBL_DEV = 1024
LANES = 128
SUBS = 8
MESH = pl.DeviceIdType.MESH


def cos_sin(phase, grid_size):
    quarter = grid_size // 4
    shift = quarter.bit_length() - 1
    quad = (phase + quarter // 2) >> shift
    r = (phase - (quad << shift)).astype(jnp.float32) * (2.0 * math.pi / grid_size)
    r2 = r * r
    s = r * (1.0 + r2 * (-1 / 6 + r2 * (1 / 120 + r2 * (-1 / 5040 + r2 * (1 / 362880)))))
    c = 1.0 + r2 * (-0.5 + r2 * (1 / 24 + r2 * (-1 / 720 + r2 * (1 / 40320))))
    swap = (quad & 1) == 1
    sine = jnp.where(swap, c, s)
    cosine = jnp.where(swap, s, c)
    sine = jnp.where((quad & 2) == 2, -sine, sine)
    cosine = jnp.where(((quad + 1) & 2) == 2, -cosine, cosine)
    return cosine, sine


def kernel(
    dims,
    x_ref, q_ref, live_ref, bands_ref, prob_ref, w_ref,
    wh_hbm, wl_hbm, tw_hbm, cot_hbm,
    contrib_ref, share_ref,
    wh, wl, tw, cot, lhs_h, lhs_l, part, rs_buf, tabs, share_buf, share_send,
    const_sem, send_sem, rs_sem, ag_sem, sh_send_sem, sh_sem,
):
    grid_size, n_sector, n_obl, scen, sec_local = dims
    n_dev = n_sector * n_obl
    me_s = lax.axis_index("sector")
    me_o = lax.axis_index("obl")
    me = me_s * n_obl + me_o
    rows = x_ref.shape[2]
    a_count = rows // sec_local
    groups = rows // SUBS
    v_groups = BANDS // LANES
    row_groups = scen * sec_local // SUBS
    tiles = v_groups * row_groups
    own = tiles // n_obl
    c_per = SUBS // sec_local

    const_copies = [
        pltpu.make_async_copy(cot_hbm.at[me_o], cot, const_sem.at[0]),
        pltpu.make_async_copy(wh_hbm, wh, const_sem.at[1]),
        pltpu.make_async_copy(wl_hbm, wl, const_sem.at[2]),
        pltpu.make_async_copy(tw_hbm.at[me_o], tw, const_sem.at[3]),
    ]
    for copy in const_copies:
        copy.start()

    barrier = pltpu.get_barrier_semaphore()

    def greet(d, carry):
        peer = lax.rem(me + d, n_dev)
        pl.semaphore_signal(
            barrier, inc=1, device_id=(peer // n_obl, lax.rem(peer, n_obl)), device_id_type=MESH
        )
        return carry

    lax.fori_loop(1, n_dev, greet, 0)

    sub = lax.broadcasted_iota(jnp.int32, (SUBS, LANES), 0)
    lane = lax.broadcasted_iota(jnp.int32, (SUBS, LANES), 1)

    const_copies[0].wait()
    sub_a = lax.broadcasted_iota(jnp.int32, (rows, LANES), 0) // sec_local
    freq = me_o * (a_count * LANES) + sub_a * LANES + lax.broadcasted_iota(
        jnp.int32, (rows, LANES), 1
    )
    first = (freq == 0).astype(jnp.float32)
    half = (1.0 - first) * (0.5 / grid_size)

    def prepare(c, carry):
        p = q_ref[c] - BANDS
        cosine, sine = cos_sin((freq * p) & (grid_size - 1), grid_size)
        gc = cot[...]
        xr = x_ref[0, c]
        xi = x_ref[1, c]
        sr = xr * half - xi * gc
        si = xr * gc + xi * half
        yr = sr * cosine - si * sine
        yi = sr * sine + si * cosine
        rh = yr.astype(jnp.bfloat16)
        ih = yi.astype(jnp.bfloat16)
        rl = (yr - rh.astype(jnp.float32)).astype(jnp.bfloat16)
        il = (yi - ih.astype(jnp.float32)).astype(jnp.bfloat16)
        lhs_h[c, 0:rows, 0:LANES] = rh
        lhs_h[c, 0:rows, LANES:] = ih
        lhs_h[c, rows:, 0:LANES] = ih
        lhs_h[c, rows:, LANES:] = -rh
        lhs_l[c, 0:rows, 0:LANES] = rl
        lhs_l[c, 0:rows, LANES:] = il
        lhs_l[c, rows:, 0:LANES] = il
        lhs_l[c, rows:, LANES:] = -rl
        return carry

    lax.fori_loop(0, scen, prepare, 0)
    for copy in const_copies[1:]:
        copy.wait()

    v_step = 256
    tw_period = tw.shape[2]
    odd = (sub & (sec_local - 1)) == (sub // c_per)

    def transform(c, carry):
        p = q_ref[c] - BANDS
        xr = x_ref[0, c]
        xi = x_ref[1, c]
        sr = xr * half - xi * cot[...]
        offset = -sr.reshape(groups, SUBS, LANES).sum(axis=0)
        offset = jnp.sum(offset, axis=1, keepdims=True)
        zero = jnp.sum((xr * first)[0:SUBS], axis=1, keepdims=True) * (1.0 / grid_size)
        for v0 in range(0, BANDS, v_step):
            def dot(left, right):
                return jnp.dot(
                    left[c], right[:, v0:v0 + v_step], preferred_element_type=jnp.float32
                )
            field = dot(lhs_h, wh) + dot(lhs_h, wl) + dot(lhs_l, wh)
            t0 = v0 % tw_period
            turned = (
                field[0:rows] * tw[0, :, t0:t0 + v_step] - field[rows:] * tw[1, :, t0:t0 + v_step]
            )
            total = turned.reshape(groups, SUBS, v_step).sum(axis=0)
            for v in range(v_step // LANES):
                vg = v0 // LANES + v
                piece = total[:, v * LANES:(v + 1) * LANES]
                left_over = (grid_size - p - vg * LANES - lane).astype(jnp.float32)
                piece = piece + offset + zero * left_over
                shift = sec_local
                while shift < SUBS:
                    piece = piece + pltpu.roll(piece, shift, 0)
                    shift *= 2
                piece = jnp.where(odd, piece, pltpu.roll(piece, 1, 0))
                tile = vg * row_groups + c // c_per
                mask = (sub & (c_per - 1)) == lax.rem(c, c_per)
                part[tile] = jnp.where(mask, piece, part[tile])
        return carry

    part[...] = jnp.zeros_like(part)
    lax.fori_loop(0, scen, transform, 0)

    pl.semaphore_wait(barrier, n_dev - 1)

    def rs_copy(d):
        peer = lax.rem(me_o + d, n_obl)
        return pltpu.make_async_remote_copy(
            src_ref=part.at[pl.ds(peer * own, own)],
            dst_ref=rs_buf.at[me_o],
            send_sem=send_sem.at[0],
            recv_sem=rs_sem.at[d],
            device_id=(me_s, peer),
            device_id_type=MESH,
        )

    for d in range(1, n_obl):
        rs_copy(d).start()
    rs_buf[me_o] = part[pl.ds(me_o * own, own)]
    for d in range(1, n_obl):
        rs_copy(d).wait_recv()
    total = rs_buf[0]
    for i in range(1, n_obl):
        total = total + rs_buf[i]
    tabs[me_s, pl.ds(me_o * own, own)] = total

    def ag_copy(d):
        peer = lax.rem(me + d, n_dev)
        mine = tabs.at[me_s, pl.ds(me_o * own, own)]
        return pltpu.make_async_remote_copy(
            src_ref=mine,
            dst_ref=mine,
            send_sem=send_sem.at[1],
            recv_sem=ag_sem.at[d],
            device_id=(peer // n_obl, lax.rem(peer, n_obl)),
            device_id_type=MESH,
        )

    def each(copy_of, method, count):
        def step(d, carry):
            getattr(copy_of(d), method)()
            return carry
        lax.fori_loop(1, count, step, 0)

    each(ag_copy, "start", n_dev)
    each(ag_copy, "wait_recv", n_dev)

    live = live_ref[0, 0]
    cap_groups = bands_ref.shape[0]
    share_send[...] = jnp.zeros_like(share_send)
    high = sub >= c_per

    def look(g, carry):
        start = pl.multiple_of(g * LANES, LANES)
        band = jnp.broadcast_to(bands_ref[pl.ds(g, 1), :], (SUBS, LANES))
        prob = jnp.broadcast_to(prob_ref[pl.ds(g, 1), :], (SUBS, LANES))
        ok = (start + lane) < live
        band = jnp.where(ok, band, 1)
        amount = jnp.where(ok, prob * band.astype(jnp.float32) * (1.0 / 256.0), 0.0)
        at = BANDS - band
        low = at & (LANES - 1)
        top = at // LANES
        masks = [top == i for i in range(1, v_groups)]
        sums = [jnp.zeros((SUBS, LANES), jnp.float32) for _ in range(row_groups)]
        for s in range(n_sector):
            w0 = jnp.broadcast_to(w_ref[pl.ds(s * sec_local, 1), pl.ds(start, LANES)], (SUBS, LANES))
            w1 = jnp.broadcast_to(
                w_ref[pl.ds(s * sec_local + 1, 1), pl.ds(start, LANES)], (SUBS, LANES)
            )
            scaled = jnp.where(high, w1, w0).astype(jnp.float32) * amount
            for r in range(row_groups):
                found = jnp.take_along_axis(tabs[s, r], low, axis=1)
                for i in range(1, v_groups):
                    found = jnp.where(
                        masks[i - 1],
                        jnp.take_along_axis(tabs[s, i * row_groups + r], low, axis=1),
                        found,
                    )
                product = scaled * found
                share_send[s, r] += product
                sums[r] = sums[r] + product
        sums = [x + pltpu.roll(x, c_per, 0) for x in sums]
        contrib_ref[:, pl.ds(start, LANES)] = jnp.where(high, sums[1], sums[0])
        return carry

    lax.fori_loop(0, cap_groups, look, 0)

    for s in range(n_sector):
        packed = jnp.zeros((SUBS, LANES), jnp.float32)
        for r in range(row_groups):
            packed = jnp.where(lane == r, jnp.sum(share_send[s, r], axis=1, keepdims=True), packed)
        share_send[s, 0] = packed

    def sh_copy(d):
        peer = lax.rem(me + d, n_dev)
        peer_s = peer // n_obl
        return pltpu.make_async_remote_copy(
            src_ref=share_send.at[peer_s, 0],
            dst_ref=share_buf.at[me],
            send_sem=sh_send_sem,
            recv_sem=sh_sem.at[d],
            device_id=(peer_s, lax.rem(peer, n_obl)),
            device_id_type=MESH,
        )

    each(sh_copy, "start", n_dev)
    share_buf[me] = share_send[me_s, 0]
    each(sh_copy, "wait_recv", n_dev)
    share_ref[...] = jnp.sum(share_buf[...], axis=0)

    for d in range(1, n_obl):
        rs_copy(d).wait_send()
    each(ag_copy, "wait_send", n_dev)
    each(sh_copy, "wait_send", n_dev)


@functools.lru_cache(None)
def constants(grid_size, n_obl, sec_local):
    per_dev = grid_size // n_obl
    n_a = grid_size // LANES
    b = np.arange(LANES)
    v = np.arange(BANDS)
    angle = 2.0 * np.pi * (b[:, None] * v[None, :] % grid_size) / grid_size
    w = np.concatenate([np.cos(angle), -np.sin(angle)], axis=0).astype(np.float32)
    wh = w.astype(jnp.bfloat16)
    wl = (w - wh.astype(np.float32)).astype(jnp.bfloat16)
    period = min(n_a, BANDS)
    a = np.arange(n_a)
    turn = 2.0 * np.pi * (a[:, None] * np.arange(period)[None, :] % n_a) / n_a
    tw = np.stack([np.cos(turn), np.sin(turn)]).astype(np.float32)
    j = np.arange(grid_size, dtype=np.float64)
    cot = np.zeros(grid_size)
    cot[1:] = 0.5 / np.tan(np.pi * j[1:] / grid_size) / grid_size
    cot = cot.reshape(n_obl, per_dev // LANES, LANES).astype(np.float32)
    return wh, wl, tw, cot


def on_device(spectrum, quantile_index, bands, default_prob, weights, live_rows):
    _, scen, sec_local, per_dev = spectrum.shape
    n_obl = lax.axis_size("obl")
    n_sector = lax.axis_size("sector")
    n_dev = n_obl * n_sector
    grid_size = per_dev * n_obl
    a_count = per_dev // LANES
    rows = a_count * sec_local
    row_groups = scen * sec_local // SUBS
    tiles = BANDS // LANES * row_groups
    cap = bands.shape[0]
    wh, wl, tw, cot = constants(grid_size, n_obl, sec_local)
    period = tw.shape[2]
    tw = np.repeat(tw.reshape(2, n_obl, a_count, period).transpose(1, 0, 2, 3), sec_local, axis=2)
    cot = np.repeat(cot, sec_local, axis=1)
    x = spectrum.reshape(2, scen, sec_local, a_count, LANES)
    x = x.transpose(0, 1, 3, 2, 4).reshape(2, scen, rows, LANES)
    vmem = pl.BlockSpec(memory_space=pltpu.VMEM)
    smem = pl.BlockSpec(memory_space=pltpu.SMEM)
    hbm = pl.BlockSpec(memory_space=pl.ANY)
    f32, bf16 = jnp.float32, jnp.bfloat16
    contrib, share = pl.pallas_call(
        functools.partial(kernel, (grid_size, n_sector, n_obl, scen, sec_local)),
        out_shape=(
            jax.ShapeDtypeStruct((scen, cap), f32),
            jax.ShapeDtypeStruct((SUBS, LANES), f32),
        ),
        in_specs=[vmem, smem, smem, vmem, vmem, vmem, hbm, hbm, hbm, hbm],
        out_specs=(vmem, vmem),
        scratch_shapes=[
            pltpu.VMEM((2 * LANES, BANDS), bf16),
            pltpu.VMEM((2 * LANES, BANDS), bf16),
            pltpu.VMEM((2, rows, period), f32),
            pltpu.VMEM((rows, LANES), f32),
            pltpu.VMEM((scen, 2 * rows, 2 * LANES), bf16),
            pltpu.VMEM((scen, 2 * rows, 2 * LANES), bf16),
            pltpu.VMEM((tiles, SUBS, LANES), f32),
            pltpu.VMEM((n_obl, tiles // n_obl, SUBS, LANES), f32),
            pltpu.VMEM((n_sector, tiles, SUBS, LANES), f32),
            pltpu.VMEM((n_dev, SUBS, LANES), f32),
            pltpu.VMEM((n_sector, row_groups, SUBS, LANES), f32),
            pltpu.SemaphoreType.DMA((4,)),
            pltpu.SemaphoreType.DMA((2,)),
            pltpu.SemaphoreType.DMA((n_obl,)),
            pltpu.SemaphoreType.DMA((n_dev,)),
            pltpu.SemaphoreType.DMA,
            pltpu.SemaphoreType.DMA((n_dev,)),
        ],
        compiler_params=pltpu.CompilerParams(collective_id=0, has_side_effects=True),
    )(
        x, quantile_index, live_rows,
        bands.reshape(cap // LANES, LANES), default_prob.reshape(cap // LANES, LANES), weights,
        wh, wl, tw, cot,
    )
    obligors = OBL_DEV * n_sector * n_obl
    sectors = weights.shape[0]
    share = share[:, :row_groups].reshape(sec_local, SUBS // sec_local, row_groups)
    share = share.transpose(2, 1, 0).reshape(scen, sec_local)
    return contrib, share * (sectors / obligors)


def solution(mesh):
    in_specs = (
        P(None, None, "sector", "obl"),
        P(),
        P(("sector", "obl")),
        P(("sector", "obl")),
        P(None, ("sector", "obl")),
        P("sector", "obl"),
    )
    out_specs = (P(None, ("sector", "obl")), P(None, "sector"))
    return jax.shard_map(
        on_device, mesh=mesh, in_specs=in_specs, out_specs=out_specs, check_vma=False
    )
```

time: 130 us -> 39.9 us (0.31)
  blocking collectives: 45.5 us -> 0 us
  Pallas kernels: 0 us -> 35.4 us
  local copies, waits for them, and re-layouts: 31.5 us -> 2.31 us
  waiting for transfers between devices: 20.8 us -> 0 us
  matrix products: 18.1 us -> 0 us
  starting transfers between devices: 6.35 us -> 0 us
  other arithmetic: 4.68 us -> 0.69 us
    pallas_call x0 -> x1, Pallas kernels: none -> 35.4 us  [on_device(): pl.pallas_call(functools.partial(kernel, (grid_size, n_sector, n_obl, sce...]
    all_gather x2 -> x0, blocking collectives: 23 us -> none  [the longest x1 14 us: on_device(): lax.all_gather(my_tables, 'obl', axis=0, tiled=True)]
    all_to_all x1 -> x0, waiting for transfers between devices: 20.8 us -> none  [on_device(): lax.all_to_all(flat_spectra, 'obl', split_axis=1, concat_axis=2, tiled=True)]
    dot_general x15 -> x0, matrix products: 18.1 us -> none  [the longest x8 7.05 us: block_step(): jnp.dot(flat_tables, one_hot, precision=highest)]
    gather x2 -> x0, local copies, waits for them, and re-layouts: 17.7 us -> none  [whole_rows(): window = jnp.take_along_axis(loss_field, index_table, axis=1)]
    psum x1 -> x0, blocking collectives: 13.6 us -> none  [on_device(): sector_total = lax.psum(sector_part, 'obl')]
    unnamed x1 -> x0, blocking collectives: 8.9 us -> none
    all_to_all x1 -> x0, starting transfers between devices: 6.35 us -> none  [on_device(): lax.all_to_all(flat_spectra, 'obl', split_axis=1, concat_axis=2, tiled=True)]
  transfers between devices with their start and end apart: 1 -> 0, of which waited for: 1 -> 0; matrix products, arithmetic and copies ran while one was open for 3% -> 0% of each run, Pallas kernels for 0% -> 0%
where the time goes in v1:
time: 39.9 us; the launch traced here: 39.7 us
  Pallas kernels  35.4 us (89%)
  local copies, waits for them, and re-layouts  2.31 us (6%)
  between operations  1.29 us (3%)
  other arithmetic  0.69 us (2%)
    pallas_call x1, Pallas kernels, on_device(): pl.pallas_call(functools.partial(kernel, (grid_size, n_sector, n_obl, sce...  35.4 us
    unnamed x1, local copies, waits for them, and re-layouts  1.57 us

profile of v1, /device:TPU:0, one launch (start us, length us, event | category | flops | bytes accessed | tf_op | source)
XLA Modules:
  0.0 39.7 jit_solution(12555227387445398015)
XLA Ops:
  1.3 35.4 %shard_map.113 = (f32[8,4096]{1,0:T(8,128)}, f32[8,128]{1,0:T(8,128)}) custom-call(f32[2,8,128,128]{3,2,1,0:T(8,128)} %bitcast.12, s32[8]{0:T(128)} %q_ref.1, s32[1,1]{1,0:T(1,128)S(6)} %copy.18.live_ref, s32[32,128]{1,0:T(8,128)} %bitcast.13, f32[32,128]{1,0:T(8,128)} %bitcast.14, s32[8,4096]{1,0:T(8,128)} %w_ref.1, ...), custom_call_target="tpu_custom_call" | custom-call | tf_op jit(solution)/shard_map/pallas_call | solution.py:312
  36.7 0.7 %slice_multiply_fusion = f32[8,2]{1,0:T(8,128)S(1)} fusion(f32[8,128]{1,0:T(8,128)} %get-tuple-element.5), kind=kLoop, calls=%fused_computation | loop fusion | flops 16 | bytes 128 | tf_op jit(solution)/shard_map/mul | solution.py:349
  37.4 0.1 copy.16
  37.5 0.6 %mul.15 = f32[8,2]{0,1:T(2,128)} reshape(f32[2,4,2]{1,0,2:T(2,128)S(1)} %bitcast.16) | data formatting | bytes 128 | tf_op jit(solution)/shard_map/mul | solution.py:349
  38.1 1.6 %copy.19 = f32[8,4096]{1,0:T(8,128)} copy(f32[8,4096]{1,0:T(8,128)} %get-tuple-element.8) | data formatting | bytes 262144

commit v2 on v1

v2 whole, which is shorter than its diff:
```python
import functools
import math

import jax
import jax.numpy as jnp
import numpy as np
from jax import lax
from jax.experimental import pallas as pl
from jax.experimental.pallas import tpu as pltpu
from jax.sharding import PartitionSpec as P

BANDS = 1024
OBL_DEV = 1024
LANES = 128
SUBS = 8
MESH = pl.DeviceIdType.MESH


def cos_sin(phase, grid_size):
    quarter = grid_size // 4
    shift = quarter.bit_length() - 1
    quad = (phase + quarter // 2) >> shift
    r = (phase - (quad << shift)).astype(jnp.float32) * (2.0 * math.pi / grid_size)
    r2 = r * r
    s = r * (1.0 + r2 * (-1 / 6 + r2 * (1 / 120 + r2 * (-1 / 5040 + r2 * (1 / 362880)))))
    c = 1.0 + r2 * (-0.5 + r2 * (1 / 24 + r2 * (-1 / 720 + r2 * (1 / 40320))))
    swap = (quad & 1) == 1
    sine = jnp.where(swap, c, s)
    cosine = jnp.where(swap, s, c)
    sine = jnp.where((quad & 2) == 2, -sine, sine)
    cosine = jnp.where(((quad + 1) & 2) == 2, -cosine, cosine)
    return cosine, sine


def kernel(
    dims,
    x_hbm, q_ref, live_ref, bands_hbm, prob_hbm, w_hbm, wh_hbm, wl_hbm, cot_hbm,
    contrib_ref, share_ref,
    x_ref, bands_ref, prob_ref, w_ref, rhs, tw, cot, lhs, part, rs_buf, tabs, hist_send, hist_buf,
    in_sem, x_sem, send_sem, rs_sem, ag_sem, sh_sem,
):
    grid_size, n_sector, n_obl, scen, sec_local = dims
    n_dev = n_sector * n_obl
    me_s = lax.axis_index("sector")
    me_o = lax.axis_index("obl")
    me = me_s * n_obl + me_o
    rows = x_ref.shape[2]
    a_count = rows // sec_local
    groups = rows // SUBS
    v_groups = BANDS // LANES
    row_groups = scen * sec_local // SUBS
    tiles = v_groups * row_groups
    own = tiles // n_obl
    c_per = SUBS // sec_local
    depth = 2 * LANES

    cot_copy = pltpu.make_async_copy(cot_hbm.at[me_o], cot, in_sem.at[0])
    x_copies = [
        pltpu.make_async_copy(x_hbm.at[:, pl.ds(h * (scen // 2), scen // 2)],
                              x_ref.at[:, pl.ds(h * (scen // 2), scen // 2)], x_sem.at[h])
        for h in range(2)
    ]
    rhs_copies = [
        pltpu.make_async_copy(wh_hbm, rhs.at[pl.ds(0, depth)], in_sem.at[1]),
        pltpu.make_async_copy(wl_hbm, rhs.at[pl.ds(depth, depth)], in_sem.at[2]),
    ]
    slot_copies = [
        pltpu.make_async_copy(bands_hbm, bands_ref, in_sem.at[3]),
        pltpu.make_async_copy(prob_hbm, prob_ref, in_sem.at[4]),
        pltpu.make_async_copy(w_hbm, w_ref, in_sem.at[5]),
    ]
    for copy in [cot_copy, *x_copies, *rhs_copies, *slot_copies]:
        copy.start()

    steps = [(ds, do) for ds in range(n_sector) for do in range(n_obl) if ds or do]
    steps.sort(key=lambda t: -(min(t[1], n_obl - t[1]) + min(t[0], n_sector - t[0])))

    def each(act, unrolled=n_dev <= 64):
        if unrolled:
            for ds, do in steps:
                act(ds, do)
        else:
            def step(d, carry):
                act(d // n_obl, lax.rem(d, n_obl))
                return carry
            lax.fori_loop(1, n_dev, step, 0)

    def peer_of(ds, do):
        return lax.rem(me_s + ds, n_sector), lax.rem(me_o + do, n_obl)

    barrier = pltpu.get_barrier_semaphore()
    each(lambda ds, do: pl.semaphore_signal(
        barrier, inc=1, device_id=peer_of(ds, do), device_id_type=MESH))

    sub = lax.broadcasted_iota(jnp.int32, (SUBS, LANES), 0)
    lane = lax.broadcasted_iota(jnp.int32, (SUBS, LANES), 1)

    tw_period = tw.shape[2]
    row_a = lax.broadcasted_iota(jnp.int32, (rows, LANES), 0) // sec_local + me_o * a_count
    row_lane = lax.broadcasted_iota(jnp.int32, (rows, LANES), 1)
    for v in range(tw_period // LANES):
        cosine, sine = cos_sin(
            (row_a * (row_lane + v * LANES)) & (tw_period - 1), tw_period
        )
        tw[0, :, v * LANES:(v + 1) * LANES] = cosine
        tw[1, :, v * LANES:(v + 1) * LANES] = sine

    freq = row_a * LANES + row_lane
    first = (freq == 0).astype(jnp.float32)
    half = (1.0 - first) * (0.5 / grid_size)

    def prepare(c, carry):
        p = q_ref[c] - BANDS
        cosine, sine = cos_sin((freq * p) & (grid_size - 1), grid_size)
        gc = cot[...]
        xr = x_ref[0, c]
        xi = x_ref[1, c]
        sr = xr * half - xi * gc
        si = xr * gc + xi * half
        yr = sr * cosine - si * sine
        yi = sr * sine + si * cosine
        rh = yr.astype(jnp.bfloat16)
        ih = yi.astype(jnp.bfloat16)
        rl = (yr - rh.astype(jnp.float32)).astype(jnp.bfloat16)
        il = (yi - ih.astype(jnp.float32)).astype(jnp.bfloat16)
        for k, (re, im) in enumerate(((rh, ih), (rh, ih), (rl, il))):
            at = k * depth
            lhs[c, 0:rows, at:at + LANES] = re
            lhs[c, 0:rows, at + LANES:at + depth] = im
            lhs[c, rows:, at:at + LANES] = im
            lhs[c, rows:, at + LANES:at + depth] = -re
        return carry

    cot_copy.wait()
    for h in range(2):
        x_copies[h].wait()
        lax.fori_loop(h * (scen // 2), (h + 1) * (scen // 2), prepare, 0)
    for copy in rhs_copies:
        copy.wait()
    rhs[2 * depth:, :] = rhs[0:depth, :]

    v_step = 256
    odd = (sub & (sec_local - 1)) == (sub // c_per)

    def transform(rg, carry):
        ends = []
        for i in range(c_per):
            c = rg * c_per + i
            xr = x_ref[0, c]
            sr = xr * half - x_ref[1, c] * cot[...]
            offset = -sr.reshape(groups, SUBS, LANES).sum(axis=0)
            offset = jnp.sum(offset, axis=1, keepdims=True)
            zero = jnp.sum((xr * first)[0:SUBS], axis=1, keepdims=True) * (1.0 / grid_size)
            ends.append((offset, zero, q_ref[c] - BANDS))
        left = lhs[pl.ds(rg * c_per, c_per)].reshape(c_per * 2 * rows, 3 * depth)
        for v0 in range(0, BANDS, v_step):
            field = jnp.dot(left, rhs[:, v0:v0 + v_step], preferred_element_type=jnp.float32)
            t0 = v0 % tw_period
            tile_of = [jnp.zeros((SUBS, LANES), jnp.float32)] * (v_step // LANES)
            for i in range(c_per):
                offset, zero, p = ends[i]
                at = i * 2 * rows
                turned = (
                    field[at:at + rows] * tw[0, :, t0:t0 + v_step]
                    - field[at + rows:at + 2 * rows] * tw[1, :, t0:t0 + v_step]
                )
                total = turned.reshape(groups, SUBS, v_step).sum(axis=0)
                for v in range(v_step // LANES):
                    piece = total[:, v * LANES:(v + 1) * LANES]
                    left_over = (grid_size - p - v0 - v * LANES - lane).astype(jnp.float32)
                    piece = piece + offset + zero * left_over
                    shift = sec_local
                    while shift < SUBS:
                        piece = piece + pltpu.roll(piece, shift, 0)
                        shift *= 2
                    piece = jnp.where(odd, piece, pltpu.roll(piece, 1, 0))
                    tile_of[v] = jnp.where((sub & (c_per - 1)) == i, piece, tile_of[v])
            for v in range(v_step // LANES):
                part[(v0 // LANES + v) * row_groups + rg] = tile_of[v]
        return carry

    lax.fori_loop(0, row_groups, transform, 0)

    pl.semaphore_wait(barrier, n_dev - 1)

    def rs_copy(d):
        peer = lax.rem(me_o + d, n_obl)
        return pltpu.make_async_remote_copy(
            src_ref=part.at[pl.ds(peer * own, own)],
            dst_ref=rs_buf.at[me_o],
            send_sem=send_sem.at[0],
            recv_sem=rs_sem.at[d],
            device_id=(me_s, peer),
            device_id_type=MESH,
        )

    for d in sorted(range(1, n_obl), key=lambda d: -min(d, n_obl - d)):
        rs_copy(d).start()
    rs_buf[me_o] = part[pl.ds(me_o * own, own)]
    for d in range(1, n_obl):
        rs_copy(d).wait_recv()
    total = rs_buf[0]
    for i in range(1, n_obl):
        total = total + rs_buf[i]
    tabs[me_s, pl.ds(me_o * own, own)] = total

    def ag_copy(ds, do):
        mine = tabs.at[me_s, pl.ds(me_o * own, own)]
        return pltpu.make_async_remote_copy(
            src_ref=mine,
            dst_ref=mine,
            send_sem=send_sem.at[1],
            recv_sem=ag_sem.at[ds * n_obl + do],
            device_id=peer_of(ds, do),
            device_id_type=MESH,
        )

    each(lambda ds, do: ag_copy(ds, do).start())

    for copy in slot_copies:
        copy.wait()
    live = live_ref[0, 0]
    cap_groups = bands_ref.shape[0]

    def slots(g, size):
        band = bands_ref[pl.ds(g, 1), :]
        prob = prob_ref[pl.ds(g, 1), :]
        ok = (g * LANES + lax.broadcasted_iota(jnp.int32, (1, LANES), 1)) < live
        band = jnp.where(ok, band, 1)
        amount = jnp.where(ok, prob * band.astype(jnp.float32) * (1.0 / 256.0), 0.0)
        return jnp.broadcast_to(BANDS - band, (size, LANES)), amount

    def count(g, sums):
        ats, lefts = [], []
        for i in range(2):
            at, amount = slots(2 * g + i, BANDS)
            start = pl.multiple_of((2 * g + i) * LANES, LANES)
            scaled = w_ref[:, pl.ds(start, LANES)].astype(jnp.float32) * amount
            split = []
            for _ in range(3):
                piece = scaled.astype(jnp.bfloat16).astype(jnp.float32)
                split.append(piece)
                scaled = scaled - piece
            lefts.append(jnp.concatenate(split, axis=0))
            ats.append(at)
        at = jnp.concatenate(ats, axis=1)
        left = jnp.concatenate(lefts, axis=1).astype(jnp.bfloat16)
        spot = lax.broadcasted_iota(jnp.int32, (BANDS, 2 * LANES), 0)
        hot = jnp.where(at == spot, 1.0, 0.0).astype(jnp.bfloat16)
        return sums + lax.dot_general(
            left, hot, (((1,), (1,)), ((), ())), preferred_element_type=jnp.float32
        )

    sectors = w_ref.shape[0]
    sums = jnp.zeros((3 * sectors, BANDS), jnp.float32)
    sums = lax.fori_loop(0, cap_groups // 2, count, sums)
    hist = sums[0:sectors] + sums[sectors:2 * sectors] + sums[2 * sectors:]
    for s in range(n_sector):
        hist_send[s] = hist[s * sec_local:(s + 1) * sec_local]

    def sh_copy(ds, do):
        peer = peer_of(ds, do)
        return pltpu.make_async_remote_copy(
            src_ref=hist_send.at[peer[0]],
            dst_ref=hist_buf.at[me],
            send_sem=send_sem.at[2],
            recv_sem=sh_sem.at[ds * n_obl + do],
            device_id=peer,
            device_id_type=MESH,
        )

    each(lambda ds, do: sh_copy(ds, do).start())
    hist_buf[me] = hist_send[me_s]
    each(lambda ds, do: ag_copy(ds, do).wait_recv())

    high = sub >= c_per

    def look(g, carry):
        start = pl.multiple_of(g * LANES, LANES)
        at, amount = slots(g, SUBS)
        amount = jnp.broadcast_to(amount, (SUBS, LANES))
        low = at & (LANES - 1)
        top = at // LANES
        masks = [top == i for i in range(1, v_groups)]
        sums = [jnp.zeros((SUBS, LANES), jnp.float32) for _ in range(row_groups)]
        for s in range(n_sector):
            w0, w1 = (
                jnp.broadcast_to(
                    w_ref[pl.ds(s * sec_local + k, 1), pl.ds(start, LANES)], (SUBS, LANES)
                )
                for k in range(2)
            )
            scaled = jnp.where(high, w1, w0).astype(jnp.float32) * amount
            for r in range(row_groups):
                found = jnp.take_along_axis(tabs[s, r], low, axis=1)
                for i in range(1, v_groups):
                    found = jnp.where(
                        masks[i - 1],
                        jnp.take_along_axis(tabs[s, i * row_groups + r], low, axis=1),
                        found,
                    )
                sums[r] = sums[r] + scaled * found
        sums = [x + pltpu.roll(x, c_per, 0) for x in sums]
        contrib_ref[:, pl.ds(start, LANES)] = jnp.where(high, sums[1], sums[0])
        return carry

    lax.fori_loop(0, cap_groups, look, 0)

    each(lambda ds, do: sh_copy(ds, do).wait_recv())
    hist = jnp.sum(hist_buf[...], axis=0)
    spread = jnp.zeros((SUBS, LANES), jnp.float32)
    for r in range(row_groups):
        total = jnp.zeros((SUBS, LANES), jnp.float32)
        for v in range(v_groups):
            h0, h1 = (
                jnp.broadcast_to(hist[k:k + 1, v * LANES:(v + 1) * LANES], (SUBS, LANES))
                for k in range(2)
            )
            total = total + tabs[me_s, v * row_groups + r] * jnp.where(high, h1, h0)
        total = jnp.sum(total, axis=1, keepdims=True)
        spread = jnp.where(lane == r * c_per + (sub & (c_per - 1)), total, spread)
    spread = spread * (sectors / (OBL_DEV * n_dev))
    for k in range(sec_local):
        row = jnp.sum(jnp.where(sub // c_per == k, spread, 0.0), axis=0, keepdims=True)
        share_ref[k:k + 1, :] = row[:, 0:scen]

    for d in range(1, n_obl):
        rs_copy(d).wait_send()
    each(lambda ds, do: ag_copy(ds, do).wait_send())
    each(lambda ds, do: sh_copy(ds, do).wait_send())


@functools.lru_cache(None)
def constants(grid_size, n_obl, sec_local):
    per_dev = grid_size // n_obl
    b = np.arange(LANES)
    v = np.arange(BANDS)
    angle = 2.0 * np.pi * (b[:, None] * v[None, :] % grid_size) / grid_size
    w = np.concatenate([np.cos(angle), -np.sin(angle)], axis=0).astype(np.float32)
    wh = w.astype(jnp.bfloat16)
    wl = (w - wh.astype(np.float32)).astype(jnp.bfloat16)
    j = np.arange(grid_size, dtype=np.float64)
    cot = np.zeros(grid_size)
    cot[1:] = 0.5 / np.tan(np.pi * j[1:] / grid_size) / grid_size
    cot = cot.reshape(n_obl, per_dev // LANES, LANES).astype(np.float32)
    return wh, wl, cot


def on_device(spectrum, quantile_index, bands, default_prob, weights, live_rows):
    _, scen, sec_local, per_dev = spectrum.shape
    n_obl = lax.axis_size("obl")
    n_sector = lax.axis_size("sector")
    n_dev = n_obl * n_sector
    grid_size = per_dev * n_obl
    a_count = per_dev // LANES
    rows = a_count * sec_local
    row_groups = scen * sec_local // SUBS
    tiles = BANDS // LANES * row_groups
    cap = bands.shape[0]
    wh, wl, cot = constants(grid_size, n_obl, sec_local)
    period = grid_size // LANES
    cot = np.repeat(cot, sec_local, axis=1)
    x = spectrum.reshape(2, scen, sec_local, a_count, LANES)
    x = x.transpose(0, 1, 3, 2, 4).reshape(2, scen, rows, LANES)
    vmem = pl.BlockSpec(memory_space=pltpu.VMEM)
    smem = pl.BlockSpec(memory_space=pltpu.SMEM)
    hbm = pl.BlockSpec(memory_space=pl.ANY)
    f32, bf16 = jnp.float32, jnp.bfloat16
    contrib, share = pl.pallas_call(
        functools.partial(kernel, (grid_size, n_sector, n_obl, scen, sec_local)),
        out_shape=(
            jax.ShapeDtypeStruct((scen, cap), f32),
            jax.ShapeDtypeStruct((sec_local, scen), f32),
        ),
        in_specs=[hbm, smem, smem, hbm, hbm, hbm, hbm, hbm, hbm],
        out_specs=(vmem, vmem),
        scratch_shapes=[
            pltpu.VMEM(x.shape, f32),
            pltpu.VMEM((cap // LANES, LANES), jnp.int32),
            pltpu.VMEM((cap // LANES, LANES), f32),
            pltpu.VMEM(weights.shape, jnp.int32),
            pltpu.VMEM((6 * LANES, BANDS), bf16),
            pltpu.VMEM((2, rows, period), f32),
            pltpu.VMEM((rows, LANES), f32),
            pltpu.VMEM((scen, 2 * rows, 6 * LANES), bf16),
            pltpu.VMEM((tiles, SUBS, LANES), f32),
            pltpu.VMEM((n_obl, tiles // n_obl, SUBS, LANES), f32),
            pltpu.VMEM((n_sector, tiles, SUBS, LANES), f32),
            pltpu.VMEM((n_sector, sec_local, BANDS), f32),
            pltpu.VMEM((n_dev, sec_local, BANDS), f32),
            pltpu.SemaphoreType.DMA((6,)),
            pltpu.SemaphoreType.DMA((2,)),
            pltpu.SemaphoreType.DMA((3,)),
            pltpu.SemaphoreType.DMA((n_obl,)),
            pltpu.SemaphoreType.DMA((n_dev,)),
            pltpu.SemaphoreType.DMA((n_dev,)),
        ],
        compiler_params=pltpu.CompilerParams(
            collective_id=0, has_side_effects=True, vmem_limit_bytes=40 * 1024 * 1024
        ),
    )(
        x, quantile_index, live_rows,
        bands.reshape(cap // LANES, LANES), default_prob.reshape(cap // LANES, LANES), weights,
        wh, wl, cot,
    )
    return contrib, share.T


def solution(mesh):
    in_specs = (
        P(None, None, "sector", "obl"),
        P(),
        P(("sector", "obl")),
        P(("sector", "obl")),
        P(None, ("sector", "obl")),
        P("sector", "obl"),
    )
    out_specs = (P(None, ("sector", "obl")), P(None, "sector"))
    return jax.shard_map(
        on_device, mesh=mesh, in_specs=in_specs, out_specs=out_specs, check_vma=False
    )
```

time: 39.9 us -> 38.5 us (0.965)
  the two profiles are of different devices: /device:TPU:0 before, /device:TPU:9 now
where the time goes in v2:
time: 38.5 us; the launch traced here: 38.1 us
  Pallas kernels  28.2 us (73%)
  local copies, waits for them, and re-layouts  8.55 us (22%)
  between operations  1.3 us (3%)
    pallas_call x1, Pallas kernels, on_device(): pl.pallas_call(functools.partial(kernel, (grid_size, n_sector, n_obl, sce...  28.2 us
    unnamed x18, local copies, waits for them, and re-layouts  8.55 us

profile of v2, /device:TPU:9, one launch (start us, length us, event | category | flops | bytes accessed | tf_op | source)
XLA Modules:
  0.0 38.1 jit_solution(2084017563369119999)
XLA Ops:
  1.3 0.0 copy-start.7
  1.3 0.6 %copy-done.7 = s32[8]{0:T(128)S(1)} copy-done((s32[8]{0:T(128)S(1)}, s32[8]{0:T(128)}, u32[]{:S(2)}) %copy-start.7) | copy-done | bytes 56
  1.9 0.0 copy-start
  1.9 1.2 %copy-done = f32[2,8,2,8192]{3,2,1,0:T(2,128)S(1)} copy-done((f32[2,8,2,8192]{3,2,1,0:T(2,128)S(1)}, f32[2,8,2,8192]{3,2,1,0:T(2,128)}, u32[]{:S(2)}) %copy-start) | copy-done | bytes 1048600
  3.2 0.0 copy-start.1
  3.2 1.0 %copy-done.1 = f32[8,128,128]{2,1,0:T(8,128)S(1)} copy-done((f32[8,128,128]{2,1,0:T(8,128)S(1)}, f32[8,128,128]{2,1,0:T(8,128)}, u32[]{:S(2)}) %copy-start.1) | copy-done | bytes 524312
  4.2 0.0 copy-start.2
  4.2 1.0 %copy-done.2 = bf16[256,1024]{1,0:T(8,128)(2,1)S(1)} copy-done((bf16[256,1024]{1,0:T(8,128)(2,1)S(1)}, bf16[256,1024]{1,0:T(8,128)(2,1)}, u32[]{:S(2)}) %copy-start.2) | copy-done | bytes 524312
  5.2 0.0 copy-start.3
  5.2 1.0 %copy-done.3 = bf16[256,1024]{1,0:T(8,128)(2,1)S(1)} copy-done((bf16[256,1024]{1,0:T(8,128)(2,1)S(1)}, bf16[256,1024]{1,0:T(8,128)(2,1)}, u32[]{:S(2)}) %copy-start.3) | copy-done | bytes 524312
  6.3 0.0 copy-start.4
  6.3 0.9 %copy-done.4 = s32[8,4096]{1,0:T(8,128)S(1)} copy-done((s32[8,4096]{1,0:T(8,128)S(1)}, s32[8,4096]{1,0:T(8,128)}, u32[]{:S(2)}) %copy-start.4) | copy-done | bytes 131096
  7.2 0.0 copy-start.5
  7.2 0.7 %copy-done.5 = s32[4096]{0:T(1024)S(1)} copy-done((s32[4096]{0:T(1024)S(1)}, s32[4096]{0:T(1024)}, u32[]{:S(2)}) %copy-start.5) | copy-done | bytes 16408
  7.9 0.0 copy-start.6
  7.9 0.7 %copy-done.6 = f32[4096]{0:T(1024)S(1)} copy-done((f32[4096]{0:T(1024)S(1)}, f32[4096]{0:T(1024)}, u32[]{:S(2)}) %copy-start.6) | copy-done | bytes 16408
  8.6 28.2 %shard_map.104 = (f32[8,4096]{1,0:T(8,128)S(1)}, f32[2,8]{1,0:T(2,128)S(1)}) custom-call(f32[2,8,128,128]{3,2,1,0:T(8,128)S(1)} %bitcast.8, s32[8]{0:T(128)S(1)} %copy-done.7, s32[1,1]{1,0:T(1,128)S(6)} %copy.14.live_ref, s32[32,128]{1,0:T(8,128)S(1)} %bitcast.9, f32[32,128]{1,0:T(8,128)S(1)} %bitcast.10, s32[8,4096]{1,0:T(8,128)S(1)} %copy-done.4, ...), custom_call_target="tpu_custom_call" | custom-call | tf_op jit(solution)/shard_map/pallas_call | solution.py:369
  36.8 0.7 %copy.15 = f32[8,4096]{1,0:T(8,128)} copy(f32[8,4096]{1,0:T(8,128)S(1)} %get-tuple-element.8) | data formatting | bytes 262144
  37.5 0.6 %copy.16 = f32[8,2]{0,1:T(2,128)} copy(f32[8,2]{0,1:T(2,128)S(1)} %bitcast.11) | data formatting | bytes 128
Async XLA Ops:
  1.3 0.7 %copy-start.7 = (s32[8]{0:T(128)S(1)}, s32[8]{0:T(128)}, u32[]{:S(2)}) copy-start(s32[8]{0:T(128)} %q_ref.1) | copy-start | bytes 100
  1.9 1.2 %copy-start = (f32[2,8,2,8192]{3,2,1,0:T(2,128)S(1)}, f32[2,8,2,8192]{3,2,1,0:T(2,128)}, u32[]{:S(2)}) copy-start(f32[2,8,2,8192]{3,2,1,0:T(2,128)} %param.9) | copy-start | bytes 3145732
  3.2 1.0 %copy-start.1 = (f32[8,128,128]{2,1,0:T(8,128)S(1)}, f32[8,128,128]{2,1,0:T(8,128)}, u32[]{:S(2)}) copy-start(f32[8,128,128]{2,1,0:T(8,128)} %constant.8.clone.cot_hbm) | copy-start | bytes 1572868
  4.2 1.0 %copy-start.2 = (bf16[256,1024]{1,0:T(8,128)(2,1)S(1)}, bf16[256,1024]{1,0:T(8,128)(2,1)}, u32[]{:S(2)}) copy-start(bf16[256,1024]{1,0:T(8,128)(2,1)} %constant.7.clone.wl_hbm) | copy-start | bytes 1572868
  5.2 1.0 %copy-start.3 = (bf16[256,1024]{1,0:T(8,128)(2,1)S(1)}, bf16[256,1024]{1,0:T(8,128)(2,1)}, u32[]{:S(2)}) copy-start(bf16[256,1024]{1,0:T(8,128)(2,1)} %constant.6.clone.wh_hbm) | copy-start | bytes 1572868
  6.3 0.9 %copy-start.4 = (s32[8,4096]{1,0:T(8,128)S(1)}, s32[8,4096]{1,0:T(8,128)}, u32[]{:S(2)}) copy-start(s32[8,4096]{1,0:T(8,128)} %w_hbm.1) | copy-start | bytes 393220
  7.2 0.7 %copy-start.5 = (s32[4096]{0:T(1024)S(1)}, s32[4096]{0:T(1024)}, u32[]{:S(2)}) copy-start(s32[4096]{0:T(1024)} %param.11) | copy-start | bytes 49156
  7.9 0.7 %copy-start.6 = (f32[4096]{0:T(1024)S(1)}, f32[4096]{0:T(1024)}, u32[]{:S(2)}) copy-start(f32[4096]{0:T(1024)} %param.12) | copy-start | bytes 49156

commit v3 on v2

--- a/solution.py
+++ b/solution.py
@@ -219,7 +219,7 @@
 
     for copy in slot_copies:
         copy.wait()
-    live = live_ref[0, 0]
+    live = live_ref[0]
     cap_groups = bands_ref.shape[0]
 
     def slots(g, size):
@@ -304,7 +304,7 @@
         contrib_ref[:, pl.ds(start, LANES)] = jnp.where(high, sums[1], sums[0])
         return carry
 
-    lax.fori_loop(0, cap_groups, look, 0)
+    lax.fori_loop(0, cap_groups, look, 0, unroll=2)
 
     each(lambda ds, do: sh_copy(ds, do).wait_recv())
     hist = jnp.sum(hist_buf[...], axis=0)
@@ -396,10 +396,10 @@
             pltpu.SemaphoreType.DMA((n_dev,)),
         ],
         compiler_params=pltpu.CompilerParams(
-            collective_id=0, has_side_effects=True, vmem_limit_bytes=40 * 1024 * 1024
+            collective_id=0, has_side_effects=True
         ),
     )(
-        x, quantile_index, live_rows,
+        x, quantile_index, live_rows.reshape(1),
         bands.reshape(cap // LANES, LANES), default_prob.reshape(cap // LANES, LANES), weights,
         wh, wl, cot,
     )

time: 38.5 us -> 31.8 us (0.83)
  the two profiles are of different devices: /device:TPU:9 before, /device:TPU:0 now
where the time goes in v3:
time: 31.8 us; the launch traced here: 31.7 us
  Pallas kernels  28.2 us (89%)
  local copies, waits for them, and re-layouts  2.13 us (7%)
  between operations  1.29 us (4%)
    pallas_call x1, Pallas kernels, on_device(): pl.pallas_call(functools.partial(kernel, (grid_size, n_sector, n_obl, sce...  28.2 us
    unnamed x4, local copies, waits for them, and re-layouts  2.13 us

profile of v3, /device:TPU:0, one launch (start us, length us, event | category | flops | bytes accessed | tf_op | source)
XLA Modules:
  0.0 31.7 jit_solution(6287365936235764315)
XLA Ops:
  1.3 28.2 %shard_map.104 = (f32[8,4096]{1,0:T(8,128)}, f32[2,8]{1,0:T(2,128)}) custom-call(f32[2,8,128,128]{3,2,1,0:T(8,128)} %bitcast.10, s32[8]{0:T(128)} %q_ref.1, s32[1]{0:T(128)} %bitcast.9.live_ref, s32[32,128]{1,0:T(8,128)} %bitcast.11, f32[32,128]{1,0:T(8,128)} %bitcast.12, s32[8,4096]{1,0:T(8,128)} %w_hbm.1, bf16[256,1024]{1,0:T(8,128)(2,1)} %constant.6.clone.wh_hbm, ...), custom_call_target="tpu_custom_call" | custom-call | tf_op jit(solution)/shard_map/pallas_call | solution.py:369
  29.5 0.0 copy-start
  29.5 1.6 %copy.15 = f32[8,4096]{1,0:T(8,128)} copy(f32[8,4096]{1,0:T(8,128)} %get-tuple-element.8) | data formatting | bytes 262144
  31.1 0.0 copy-done
  31.1 0.6 %copy.16 = f32[8,2]{0,1:T(2,128)} copy(f32[8,2]{0,1:T(2,128)S(1)} %bitcast.13) | data formatting | bytes 128
Async XLA Ops:
  29.5 1.6 %copy-start = (f32[2,8]{1,0:T(2,128)S(1)}, f32[2,8]{1,0:T(2,128)}, u32[]{:S(2)}) copy-start(f32[2,8]{1,0:T(2,128)} %get-tuple-element.5) | copy-start | bytes 196
